TPU v7x, 256 devices: a whole 4x4x8 slice. The times are simulated.
256 devices in a mesh: section: 8 (over z), ex: 4 (over x), ey: 8 (over y, core).
Axes of the slice: x: 4, y: 4, z: 8, core: 2. Of those that a mesh axis runs over, the one named last changes fastest.
Arguments:
- section_out: bfloat16 [8, 2048, 7168], P('section', ('ex', 'ey')), may hold values from -6 to 6
- expert_ids: int32 [8, 2048, 2], P('section', ('ex', 'ey')), may hold values from 0 to 7, all different within a row; in each aligned block of 64 rows (0 to 63, 64 to 127, ..., all dimensions but the last counted through in order) at most 24 rows name the same one
- gate_weights: float32 [8, 2048, 2], P('section', ('ex', 'ey')), may hold values from 0.1 to 1
- w_gate_up: bfloat16 [8, 8, 7168, 2, 1024], P('section', 'ey', None, None, 'ex'), may hold values from -0.0625 to 0.0625
- w_down: bfloat16 [8, 8, 1024, 7168], P('section', 'ey', 'ex'), may hold values from -0.1875 to 0.1875
Outputs:
- next_state: bfloat16 [8, 2048, 7168], P('section', ('ex', 'ey'))
Inputs may be any that keep to these rules, and one draw needn't show every extreme that they name: `expert_ids`: each row names 2 different experts. In the rows of one device (aligned blocks of 64 rows, all leading dimensions in order) no expert is named by more than 24 rows, and some block of every draw names one expert exactly 24 times.
All inputs are finite; a program needn't handle non-finite values.
Results may differ from a plain program's by a relative error of at most 0.008.
Values may be sent and summed in bfloat16 or wider, within the bound.
A program may use at most 128 MiB of HBM per device.

v0:
```python
import jax
import jax.numpy as jnp
from jax import lax
from jax.sharding import PartitionSpec as P


def shifted(value, axis, steps):
    count = lax.axis_size(axis)
    pairs = [(source, (source + steps) % count) for source in range(count)]
    return lax.ppermute(value, axis, pairs)


def expert_hidden(token_rows, gate_up, unit_count):
    mixed = jnp.dot(token_rows, gate_up, preferred_element_type=jnp.float32)
    return (jax.nn.silu(mixed[:, :unit_count]) * mixed[:, unit_count:]).astype(jnp.bfloat16)


def on_device(section_out, expert_ids, gate_weights, w_gate_up, w_down):
    tok_rows = section_out.shape[1]
    model_width = section_out.shape[2]
    top_count = expert_ids.shape[2]
    experts = lax.axis_size("ey")
    capacity = min(tok_rows, 3 * tok_rows * top_count // (2 * experts))
    unit_count = w_down.shape[2]
    gate_up = w_gate_up[0, 0].reshape(model_width, 2 * unit_count)
    down_rows = w_down[0, 0]
    incoming = shifted(section_out, "section", 1)[0]
    chosen = expert_ids[0].reshape(-1)
    one_hot = (chosen[:, None] == jnp.arange(experts, dtype=jnp.int32)[None, :]).astype(jnp.int32)
    slot_rank = jnp.sum((jnp.cumsum(one_hot, axis=0) - one_hot) * one_hot, axis=1)
    position = chosen * capacity + slot_rank
    token_of = jnp.arange(tok_rows * top_count, dtype=jnp.int32) // top_count
    filled = jnp.zeros((experts * capacity,), jnp.int32).at[position].set(1)
    source_row = jnp.zeros((experts * capacity,), jnp.int32).at[position].set(token_of)
    outgoing = jnp.where(filled[:, None] > 0, incoming[source_row], jnp.zeros((), jnp.bfloat16))
    arrived = lax.all_to_all(
        outgoing.reshape(experts, capacity, model_width),
        "ey",
        split_axis=0,
        concat_axis=0,
        tiled=True,
    ).reshape(experts * capacity, model_width)
    hidden_all = expert_hidden(
        lax.all_gather(arrived, "ex", axis=0, tiled=True), gate_up, unit_count
    )
    summed = lax.psum_scatter(
        jnp.dot(hidden_all, down_rows, preferred_element_type=jnp.float32).astype(jnp.bfloat16),
        "ex",
        scatter_dimension=0,
        tiled=True,
    )
    expert_out = lax.all_to_all(
        summed.reshape(experts, capacity, model_width),
        "ey",
        split_axis=0,
        concat_axis=0,
        tiled=True,
    ).reshape(experts * capacity, model_width)
    picked = expert_out[position].reshape(tok_rows, top_count, model_width)
    weighted = jnp.einsum("tkd,tk->td", picked.astype(jnp.float32), gate_weights[0])
    result = (incoming.astype(jnp.float32) + weighted).astype(jnp.bfloat16)
    return result[None]


def solution(mesh):
    return jax.shard_map(
        on_device,
        mesh=mesh,
        in_specs=(
            P("section", ("ex", "ey"), None),
            P("section", ("ex", "ey"), None),
            P("section", ("ex", "ey"), None),
            P("section", "ey", None, None, "ex"),
            P("section", "ey", "ex", None),
        ),
        out_specs=P("section", ("ex", "ey"), None),
        check_vma=False,
    )
```

profile of v0, /device:TPU:1, one launch (start us, length us, event | category | flops | bytes accessed | tf_op | source)
XLA Modules:
  0.0 363.6 jit_solution(1292893236069667634)
XLA Ops:
  6.5 0.0 all-gather.2.cloned.1.call-start
  6.5 2.5 collective-permute-start
  9.0 0.8 copy.9
  9.8 0.7 broadcast_multiply_fusion
  10.4 0.1 eq.15
  10.6 0.1 fusion.6
  10.7 0.1 copy.8
  10.8 0.1 mul.28
  10.9 0.2 reduce_window_sum.11
  11.1 0.2 select_reduce_fusion
  11.3 1.0 scatter_custom_fusion.1
  12.3 1.0 scatter_custom_fusion
  13.3 0.1 broadcast_in_dim.29
  13.4 19.8 %collective-permute-done = bf16[1,64,7168]{2,1,0:T(8,128)(2,1)S(1)} collective-permute-done((bf16[1,64,7168]{2,1,0:T(8,128)(2,1)}, bf16[1,64,7168]{2,1,0:T(8,128)(2,1)S(1)}, u32[]{:S(2)}, u32[]{:S(2)}) %collective-permute-start) | collective-permute-done | bytes 917536 | tf_op jit(solution)/shard_map/ppermute | solution.py:10
  33.2 3.8 %gather_fusion = bf16[192,7168]{1,0:T(8,128)(2,1)} fusion(bf16[64,7168]{1,0:T(8,128)(2,1)S(1)} %bitcast.32, s32[1024]{0:T(1024)S(1)} %pad_clamp_fusion.1), kind=kCustom, calls=%fused_computation | custom fusion | bytes 5505792 | tf_op jit(solution)/shard_map/gather | solution.py:35
  37.0 2.0 broadcast_select_fusion
  39.1 39.0 %all_to_all.10 = bf16[8,24,7168]{2,1,0:T(8,128)(2,1)} all-to-all(bf16[8,24,7168]{2,1,0:T(8,128)(2,1)S(1)} %broadcast_select_fusion), channel_id=1, replica_groups=mesh['section'=8,'ex'=4,'ey'=8] {'ey'}, dimensions={0} | all-to-all | bytes 5505024 | tf_op jit(solution)/shard_map/all_to_all | solution.py:36
  78.1 0.0 all-gather.2.cloned.1.call-update
  78.1 0.0 reduce-scatter.2.cloned.1.call-start
  78.1 7.4 %copy.12 = bf16[896,8,2,256]{3,1,2,0:T(8,128)(2,1)} copy(bf16[896,8,2,256]{3,2,1,0:T(2,128)(2,1)} %bitcast.35) | data formatting | bytes 14680064
  85.5 98.6 %all-gather.2.cloned.1.call-done = bf16[768,7168]{1,0:T(8,128)(2,1)} async-done(((bf16[192,7168]{1,0:T(8,128)(2,1)}), bf16[768,7168]{1,0:T(8,128)(2,1)}) %all-gather.2.cloned.1.call-update) | async-done | bytes 11010064 | tf_op jit(solution)/shard_map/all_gather | solution.py:44
  184.1 0.0 copy-start
  184.1 10.9 %fusion.13 = f32[768,512]{1,0:T(8,128)S(1)} fusion(bf16[768,7168]{1,0:T(8,128)(2,1)} %all-gather.2.cloned.1.call-done, bf16[7168,512]{1,0:T(8,128)(2,1)} %bitcast.36), kind=kOutput, calls=%fused_computation.33 | convolution fusion | flops 5637144576 | bytes 19922944 | tf_op jit(solution)/shard_map/dot_general | solution.py:14
  195.0 0.0 copy-done
  195.0 5.8 %convolution_convert_fusion = bf16[768,7168]{1,0:T(8,128)(2,1)} fusion(bf16[1,1,256,7168]{3,2,1,0:T(8,128)(2,1)S(1)} %copy-done, f32[768,512]{1,0:T(8,128)S(1)} %fusion.13), kind=kOutput, calls=%fused_computation.4 | convolution fusion | flops 2825256960 | bytes 16252928 | tf_op jit(solution)/shard_map/dot_general | solution.py:47
  200.7 0.0 reduce-scatter.2.cloned.1.call-update
  200.8 105.5 %reduce-scatter.2.cloned.1.call-done = bf16[192,7168]{1,0:T(8,128)(2,1)} async-done(((bf16[768,7168]{1,0:T(8,128)(2,1)}), bf16[192,7168]{1,0:T(8,128)(2,1)}) %reduce-scatter.2.cloned.1.call-update) | async-done | bytes 2752528 | tf_op jit(solution)/shard_map/reduce_scatter | solution.py:46
  306.3 0.0 copy-start.1
  306.3 5.1 %all-to-all-start.1 = ((bf16[8,24,7168]{2,1,0:T(8,128)(2,1)}), bf16[8,24,7168]{2,1,0:T(8,128)(2,1)}, u32[]{:S(2)}, u32[]{:S(2)}) async-start(bf16[8,24,7168]{2,1,0:T(8,128)(2,1)} %bitcast.37), calls=%async_computation.2 | async-start | bytes 5505024 | tf_op jit(solution)/shard_map/all_to_all | solution.py:52
  311.4 0.0 copy-done.1
  311.5 0.1 copy.10
  311.6 33.2 %all-to-all-done.1 = bf16[8,24,7168]{2,1,0:T(8,128)(2,1)} async-done(((bf16[8,24,7168]{2,1,0:T(8,128)(2,1)}), bf16[8,24,7168]{2,1,0:T(8,128)(2,1)}, u32[]{:S(2)}, u32[]{:S(2)}) %all-to-all-start.1) | async-done | bytes 2752544 | tf_op jit(solution)/shard_map/all_to_all | solution.py:52
  344.8 5.5 %gather_fusion.1 = bf16[128,7168]{1,0:T(8,128)(2,1)S(1)} fusion(bf16[192,7168]{1,0:T(8,128)(2,1)} %bitcast.7, s32[1024]{0:T(1024)S(1)} %pad_clamp_fusion), kind=kCustom, calls=%fused_computation.1 | custom fusion | bytes 3670528 | tf_op jit(solution)/shard_map/gather | solution.py:59
  350.3 1.7 reshape.53
  352.0 3.5 fusion.14
  355.5 1.3 fusion.2
  (7 shorter events, 0.0 us)
Async XLA Ops:
  6.5 177.5 %all-gather.2.cloned.1.call-start = ((), (), s32[]{:S(2)}) async-start(), calls=%async_computation.3 | async-start | bytes 13762560 | tf_op jit(solution)/shard_map/all_gather | solution.py:44
  6.5 26.7 %collective-permute-start = (bf16[1,64,7168]{2,1,0:T(8,128)(2,1)}, bf16[1,64,7168]{2,1,0:T(8,128)(2,1)S(1)}, u32[]{:S(2)}, u32[]{:S(2)}) collective-permute-start(bf16[1,64,7168]{2,1,0:T(8,128)(2,1)} %param.5), channel_id=1, source_target_pairs={{0,32},{32,64},{64,96},{96,128},{128,160},{160,192},{192,224},{224... | collective-permute-start | bytes 2752520 | tf_op jit(solution)/shard_map/ppermute | solution.py:10
  78.1 228.2 %reduce-scatter.2.cloned.1.call-start = ((), (), s32[]{:S(2)}) async-start(), calls=%async_computation.4 | async-start | bytes 13762560 | tf_op jit(solution)/shard_map/reduce_scatter | solution.py:46
  184.1 10.9 %copy-start = (bf16[1,1,256,7168]{3,2,1,0:T(8,128)(2,1)S(1)}, bf16[1,1,256,7168]{3,2,1,0:T(8,128)(2,1)}, u32[]{:S(2)}) copy-start(bf16[1,1,256,7168]{3,2,1,0:T(8,128)(2,1)} %param.9) | copy-start | bytes 11010052
  306.3 5.1 %copy-start.1 = (f32[1,64,2]{1,2,0:T(2,128)S(1)}, f32[1,64,2]{1,2,0:T(2,128)}, u32[]{:S(2)}) copy-start(f32[1,64,2]{1,2,0:T(2,128)} %param.7) | copy-start | bytes 1540
  306.3 38.5 %all-to-all-start.1 = ((bf16[8,24,7168]{2,1,0:T(8,128)(2,1)}), bf16[8,24,7168]{2,1,0:T(8,128)(2,1)}, u32[]{:S(2)}, u32[]{:S(2)}) async-start(bf16[8,24,7168]{2,1,0:T(8,128)(2,1)} %bitcast.37), calls=%async_computation.2 | async-start | bytes 5505024 | tf_op jit(solution)/shard_map/all_to_all | solution.py:52
Sparse Core Ops, SparseCore 0:
  78.2 105.8 all-gather.1
  200.9 105.3 reduce-scatter.1
where the time goes:
time: 364 us
  waiting for transfers between devices  257 us (71%)
  blocking collectives  39 us (11%)
  local copies, waits for them, and re-layouts  21.7 us (6%)
  matrix products  20.2 us (6%)
  between operations  13.5 us (4%)
  starting transfers between devices  7.64 us (2%)
  other arithmetic  4.43 us (1%)
    reduce_scatter x1, waiting for transfers between devices, on_device(): lax.psum_scatter(jnp.dot(hidden_all, down_rows, preferred_element_type=jn...  106 us
    all_gather x1, waiting for transfers between devices, on_device(): lax.all_gather(arrived, 'ex', axis=0, tiled=True)  98.6 us
    all_to_all x1, blocking collectives, on_device(): lax.all_to_all(outgoing.reshape(experts, capacity, model_width), 'ey', sp...  39 us
    all_to_all x1, waiting for transfers between devices, on_device(): lax.all_to_all(summed.reshape(experts, capacity, model_width), 'ey', spli...  33.2 us
    ppermute x1, waiting for transfers between devices, shifted(): return lax.ppermute(value, axis, pairs)  19.8 us
    dot_general x1, matrix products, expert_hidden(): mixed = jnp.dot(token_rows, gate_up, preferred_element_type=jnp.float32)  10.9 us
    unnamed x6, local copies, waits for them, and re-layouts  8.14 us
  transfers between devices with their start and end apart: 4, of which 4 were waited for; matrix products, arithmetic and copies ran while one was open for 3% of the time, Pallas kernels for 0%

commit v1 on v0

v1 whole, which is shorter than its diff:
```python
import jax
import jax.numpy as jnp
from jax import lax
from jax.experimental import pallas as pl
from jax.experimental.pallas import tpu as pltpu
from jax.sharding import PartitionSpec as P

MESH = pl.DeviceIdType.MESH
ROWS = 16
EXT = 128
BF = jnp.bfloat16
F32 = jnp.float32


def moe_kernel(
    sec_ref, gate_ref, wgu_hbm, wd_hbm, out_ref,
    xb, zin, ext, wgu, wd, acc, hid, part, peer, rb, tot, rb2,
    wsem, zsend, zrecv, agr, ags, prd, pds, relay, meet, rsend, relay2, meet2, rsend2, free_x, free_p,
):
    groups = zin.shape[0]
    width = zin.shape[2]
    units = wd.shape[0]
    quarter = width // 4
    half = EXT + 2 * quarter
    whole = EXT + width
    col_a, col_b = pl.ds(0, half), pl.ds(half, 2 * quarter)
    col_q = (
        pl.ds(0, EXT + quarter), pl.ds(EXT + quarter, quarter),
        pl.ds(half, quarter), pl.ds(half + quarter, quarter),
    )
    sec = lax.axis_index("section")
    x = lax.axis_index("ex")
    ey = lax.axis_index("ey")
    y, c = lax.div(ey, 2), lax.rem(ey, 2)
    co = 1 - c
    n_sec = lax.axis_size("section")
    xp, xm, xd = lax.rem(x + 1, 4), lax.rem(x + 3, 4), lax.rem(x + 2, 4)
    yp, ym, yd = lax.rem(y + 1, 4), lax.rem(y + 3, 4), lax.rem(y + 2, 4)
    zp, zm = lax.rem(sec + 1, n_sec), lax.rem(sec + n_sec - 1, n_sec)
    to_xp, to_xm = (sec, xp, ey), (sec, xm, ey)
    to_yp, to_ym = (sec, x, yp * 2 + c), (sec, x, ym * 2 + c)
    to_peer = (sec, x, y * 2 + co)
    to_zp, to_zm = (zp, x, ey), (zm, x, ey)

    def rdma(src, dst, ssem, rsem, device):
        return pltpu.make_async_remote_copy(
            src_ref=src, dst_ref=dst, send_sem=ssem, recv_sem=rsem, device_id=device, device_id_type=MESH
        )

    def wait_recv(ref, sem):
        rdma(ref, ref, sem, sem, to_peer).wait_recv()

    def wait_send(ref, sem):
        rdma(ref, ref, sem, sem, to_peer).wait_send()

    barrier = pltpu.get_barrier_semaphore()
    for device in (to_xp, to_xm, to_yp, to_ym, to_peer, to_zp, to_zm):
        pl.semaphore_signal(barrier, inc=1, device_id=device, device_id_type=MESH)
    pl.semaphore_wait(barrier, 7)

    for g in range(groups):
        rdma(sec_ref.at[pl.ds(g * ROWS, ROWS)], zin.at[g], zsend.at[g], zrecv.at[g], to_zp).start()
    load_gu = pltpu.make_async_copy(wgu_hbm, wgu, wsem.at[0])
    load_d = pltpu.make_async_copy(wd_hbm, wd, wsem.at[1])
    load_gu.start()
    load_d.start()

    gate = gate_ref[...]
    high = gate.astype(BF).astype(F32)
    mid = (gate - high).astype(BF).astype(F32)
    low = gate - high - mid
    lane = lax.broadcasted_iota(jnp.int32, gate.shape, 1)
    ext[...] = jnp.where(lane < 8, high, jnp.where(lane < 16, mid, low)).astype(BF).reshape(ext.shape)

    def gather_1(a, p):
        @pl.when(a >= 2)
        def _():
            pl.semaphore_wait(free_x.at[a - 2], 5)

        wait_recv(zin.at[a], zrecv.at[a])
        own = xb.at[p, c, y, x]
        own[:, pl.ds(0, EXT)] = ext[a]
        own[:, pl.ds(EXT, width)] = zin[a]
        own_a, own_b = own.at[:, col_a], own.at[:, col_b]
        rdma(own_a, own_a, ags.at[a, 0], agr.at[a, 0], to_xp).start()
        rdma(own_a, own_a, ags.at[a, 0], agr.at[a, 1], to_xm).start()
        rdma(own_b, own_b, ags.at[a, 0], agr.at[a, 2], to_yp).start()
        rdma(own_b, own_b, ags.at[a, 0], agr.at[a, 3], to_ym).start()
        rdma(own, own, ags.at[a, 4], agr.at[a, 16], to_peer).start()
        spread(a, p, x, y)

    def spread(a, p, bx, by):
        src_a, src_b = xb.at[p, c, y, bx, :, col_a], xb.at[p, c, by, x, :, col_b]
        rdma(src_a, src_a, ags.at[a, 2], agr.at[a, 8], to_yp).start()
        rdma(src_a, src_a, ags.at[a, 2], agr.at[a, 9], to_ym).start()
        rdma(src_b, src_b, ags.at[a, 2], agr.at[a, 10], to_xp).start()
        rdma(src_b, src_b, ags.at[a, 2], agr.at[a, 11], to_xm).start()

    def to_partner(a, ref):
        rdma(ref, ref, ags.at[a, 4], agr.at[a, 16], to_peer).start()

    def gather_2(a, p):
        left, right = xb.at[p, c, y, xm], xb.at[p, c, y, xp]
        below, above = xb.at[p, c, ym, x], xb.at[p, c, yp, x]
        wait_recv(left.at[:, col_a], agr.at[a, 0])
        rdma(left.at[:, col_q[0]], left.at[:, col_q[0]], ags.at[a, 1], agr.at[a, 4], to_xp).start()
        wait_recv(right.at[:, col_a], agr.at[a, 1])
        rdma(right.at[:, col_q[1]], right.at[:, col_q[1]], ags.at[a, 1], agr.at[a, 5], to_xm).start()
        wait_recv(below.at[:, col_b], agr.at[a, 2])
        rdma(below.at[:, col_q[2]], below.at[:, col_q[2]], ags.at[a, 1], agr.at[a, 6], to_yp).start()
        wait_recv(above.at[:, col_b], agr.at[a, 3])
        rdma(above.at[:, col_q[3]], above.at[:, col_q[3]], ags.at[a, 1], agr.at[a, 7], to_ym).start()
        spread(a, p, xm, ym)
        spread(a, p, xp, yp)
        for ref in (left.at[:, col_a], right.at[:, col_a], below.at[:, col_b], above.at[:, col_b]):
            to_partner(a, ref)

    def gather_3(a, p):
        across, over = xb.at[p, c, y, xd], xb.at[p, c, yd, x]
        wait_recv(across.at[:, col_q[0]], agr.at[a, 4])
        wait_recv(across.at[:, col_q[1]], agr.at[a, 5])
        wait_recv(over.at[:, col_q[2]], agr.at[a, 6])
        wait_recv(over.at[:, col_q[3]], agr.at[a, 7])
        spread(a, p, xd, yd)
        to_partner(a, across.at[:, col_a])
        to_partner(a, over.at[:, col_b])

    def gather_4(a, p):
        below, above = xb.at[p, c, ym], xb.at[p, c, yp]
        left, right = xb.at[p, c, :, xm], xb.at[p, c, :, xp]
        wait_recv(below.at[:, :, col_a], agr.at[a, 8])
        rdma(below.at[:, :, col_q[0]], below.at[:, :, col_q[0]], ags.at[a, 3], agr.at[a, 12], to_yp).start()
        wait_recv(above.at[:, :, col_a], agr.at[a, 9])
        rdma(above.at[:, :, col_q[1]], above.at[:, :, col_q[1]], ags.at[a, 3], agr.at[a, 13], to_ym).start()
        wait_recv(left.at[:, :, col_b], agr.at[a, 10])
        rdma(left.at[:, :, col_q[2]], left.at[:, :, col_q[2]], ags.at[a, 3], agr.at[a, 14], to_xp).start()
        wait_recv(right.at[:, :, col_b], agr.at[a, 11])
        rdma(right.at[:, :, col_q[3]], right.at[:, :, col_q[3]], ags.at[a, 3], agr.at[a, 15], to_xm).start()
        for ref in (below.at[:, :, col_a], above.at[:, :, col_a], left.at[:, :, col_b], right.at[:, :, col_b]):
            to_partner(a, ref)

    def gather_5(a, p):
        over, across = xb.at[p, c, yd], xb.at[p, c, :, xd]
        wait_recv(over.at[:, :, col_q[0]], agr.at[a, 12])
        wait_recv(over.at[:, :, col_q[1]], agr.at[a, 13])
        to_partner(a, over.at[:, :, col_a])
        wait_recv(across.at[:, :, col_q[2]], agr.at[a, 14])
        wait_recv(across.at[:, :, col_q[3]], agr.at[a, 15])
        to_partner(a, across.at[:, :, col_b])

    tokens = acc.shape[0]
    depth = quarter if quarter % 256 else quarter // 2

    def up(g, p):
        wait_recv(xb.at[p, co], agr.at[g, 16])

        def step(k, carry):
            at = pl.multiple_of(k * depth, 128)
            rows = xb[p, :, :, :, :, pl.ds(EXT + at, depth)].reshape(tokens, depth)
            term = jnp.dot(rows, wgu[pl.ds(at, depth), :], preferred_element_type=F32)
            acc[...] = jnp.where(k == 0, term, acc[...] + term)
            return carry

        lax.fori_loop(0, width // depth, step, 0)

        def activate(i, carry):
            fours = 4 * ROWS
            at = pl.multiple_of(i * fours, fours)
            coded = xb[p, lax.div(i, 4), lax.rem(i, 4), :, :, pl.ds(0, EXT)].reshape(fours, EXT).astype(F32)
            lanes = lax.broadcasted_iota(jnp.int32, coded.shape, 1)
            weight = jnp.sum(jnp.where(lax.rem(lanes, 8) == ey, coded, 0.0), axis=1, keepdims=True)
            first = acc[pl.ds(at, fours), pl.ds(0, units)]
            second = acc[pl.ds(at, fours), pl.ds(units, units)]
            value = first / (1.0 + jnp.exp(-first)) * second
            hid[pl.ds(at, fours), :] = (value * weight).astype(BF)
            return carry

        lax.fori_loop(0, tokens // (4 * ROWS), activate, 0)
        wait_send(xb.at[p, c, 0, pl.ds(0, 2)], ags.at[g, 0])
        wait_send(xb.at[p, c, 0, 0], ags.at[g, 1])
        wait_send(xb.at[p, c, pl.ds(0, 2)], ags.at[g, 2])
        wait_send(xb.at[p, c, 0], ags.at[g, 3])
        wait_send(xb.at[p, c], ags.at[g, 4])

        @pl.when(g < 2)
        def _():
            for device in (to_xp, to_xm, to_yp, to_ym, to_peer):
                pl.semaphore_signal(free_x.at[g], inc=1, device_id=device, device_id_type=MESH)

    def cols(q):
        return pl.ds(q * quarter, quarter)

    def pick(q, bx, by):
        return part.at[c, by, :, :, cols(q)] if q < 2 else part.at[c, :, bx, :, cols(q)]

    fwd = ((xp, yp), (xm, ym))
    bwd = ((xm, ym), (xp, yp))
    dev_first = ((to_yp, to_ym), (to_ym, to_yp), (to_xp, to_xm), (to_xm, to_xp))
    dev_second = ((to_xp, to_xm), (to_xm, to_xp), (to_yp, to_ym), (to_ym, to_yp))

    def wait_part(g):
        wait_send(part.at[co], pds.at[g])
        wait_send(part.at[c, pl.ds(0, 3)], rsend.at[g])

    def down(g):
        @pl.when(g >= 1)
        def _():
            wait_part(g - 1)
            pl.semaphore_wait(free_p.at[g - 1], 1)

        tile = 256
        for q in range(4):
            def step(j, carry):
                at = pl.multiple_of(q * quarter + j * tile, 128)
                value = jnp.dot(hid[...], wd[:, pl.ds(at, tile)], preferred_element_type=F32)
                part[:, :, :, :, pl.ds(at, tile)] = value.astype(BF).reshape(2, 4, 4, ROWS, tile)
                return carry

            lax.fori_loop(0, quarter // tile, step, 0)
            rdma(part.at[co, :, :, :, cols(q)], peer.at[:, :, :, cols(q)], pds.at[g], prd.at[g, q], to_peer).start()
        for q in range(4):
            wait_recv(peer.at[:, :, :, cols(q)], prd.at[g, q])

            def add(i, carry):
                iy, ix = lax.div(i, 4), lax.rem(i, 4)
                total = part[c, iy, ix, :, cols(q)].astype(F32) + peer[iy, ix, :, cols(q)].astype(F32)
                part[c, iy, ix, :, cols(q)] = total.astype(BF)
                return carry

            lax.fori_loop(0, 16, add, 0)
            k = q % 2
            rdma(pick(q, xd, yd), rb.at[g, q, 0], rsend.at[g], relay.at[g, q], dev_first[q][0]).start()
            rdma(pick(q, *bwd[k]), rb.at[g, q, 1], rsend.at[g], meet.at[g, q], dev_first[q][1]).start()

        @pl.when(g < groups - 1)
        def _():
            pl.semaphore_signal(free_p.at[g], inc=1, device_id=to_peer, device_id_type=MESH)

    def scatter_2(g):
        for q in range(4):
            wait_recv(rb.at[g, q, 0], relay.at[g, q])
            mine = pick(q, *fwd[q % 2])

            def add(i, carry):
                mine[i] = (mine[i].astype(F32) + rb[g, q, 0, i].astype(F32)).astype(BF)
                return carry

            lax.fori_loop(0, 4, add, 0)
            rdma(mine, rb.at[g, q, 2], rsend.at[g], meet.at[g, q], dev_first[q][0]).start()

    def scatter_3(g):
        for q in range(4):
            wait_recv(rb.at[g, q, pl.ds(1, 2)], meet.at[g, q])
            mine = pick(q, x, y)

            def add(i, carry):
                total = mine[i].astype(F32) + rb[g, q, 1, i].astype(F32) + rb[g, q, 2, i].astype(F32)
                tot[q, i] = total.astype(BF)
                return carry

            lax.fori_loop(0, 4, add, 0)
            k = q % 2
            far, back = (xd, bwd[k][0]) if q < 2 else (yd, bwd[k][1])
            rdma(tot.at[q, far], rb2.at[g, q, 0], rsend2.at[g], relay2.at[g, q], dev_second[q][0]).start()
            rdma(tot.at[q, back], rb2.at[g, q, 1], rsend2.at[g], meet2.at[g, q], dev_second[q][1]).start()

    def scatter_4(g):
        for q in range(4):
            wait_recv(rb2.at[g, q, 0], relay2.at[g, q])
            at = fwd[q % 2][0] if q < 2 else fwd[q % 2][1]
            tot[q, at] = (tot[q, at].astype(F32) + rb2[g, q, 0].astype(F32)).astype(BF)
            rdma(tot.at[q, at], rb2.at[g, q, 2], rsend2.at[g], meet2.at[g, q], dev_second[q][0]).start()

    def scatter_5(g):
        rows = pl.ds(pl.multiple_of(g * ROWS, ROWS), ROWS)
        for q in range(4):
            wait_recv(rb2.at[g, q, pl.ds(1, 2)], meet2.at[g, q])
            at = x if q < 2 else y
            total = tot[q, at].astype(F32) + rb2[g, q, 1].astype(F32) + rb2[g, q, 2].astype(F32)
            out_ref[rows, cols(q)] = (total + zin[g, :, cols(q)].astype(F32)).astype(BF)
        wait_send(tot.at[pl.ds(0, 3)], rsend2.at[g])

    def turn(i, carry):
        a, g, t = i, i - 1, i - 2
        pa, pg = lax.rem(a, 2), lax.rem(i + 1, 2)
        gathers = a < groups
        computes = (g >= 0) & (g < groups)
        ends = t >= 0

        @pl.when(i == 1)
        def _():
            load_gu.wait()
            load_d.wait()

        @pl.when(gathers)
        def _():
            gather_1(a, pa)

        @pl.when(computes)
        def _():
            up(g, pg)

        @pl.when(ends)
        def _():
            scatter_3(t)

        @pl.when(gathers)
        def _():
            gather_2(a, pa)

        @pl.when(computes)
        def _():
            down(g)

        @pl.when(ends)
        def _():
            scatter_4(t)

        @pl.when(gathers)
        def _():
            gather_3(a, pa)

        @pl.when(ends)
        def _():
            scatter_5(t)

        @pl.when(gathers)
        def _():
            gather_4(a, pa)

        @pl.when(computes)
        def _():
            scatter_2(g)

        @pl.when(gathers)
        def _():
            gather_5(a, pa)

        return carry

    lax.fori_loop(0, groups + 2, turn, 0)
    wait_part(groups - 1)
    for g in range(groups):
        wait_send(zin.at[g], zsend.at[g])


def on_device(section_out, expert_ids, gate_weights, w_gate_up, w_down):
    rows, width = section_out.shape[1:]
    units = w_down.shape[2]
    groups = rows // ROWS
    quarter = width // 4
    chosen = expert_ids[0][:, :, None] == jnp.arange(8, dtype=jnp.int32)[None, None, :]
    dense = jnp.sum(jnp.where(chosen, gate_weights[0][:, :, None], 0.0), axis=1)
    gates = jnp.concatenate([dense, dense, dense, jnp.zeros((rows, EXT - 24), F32)], axis=1)
    gate_up = w_gate_up[0, 0].reshape(width, 2 * units)
    hbm = pl.BlockSpec(memory_space=pl.ANY)
    vmem = pl.BlockSpec(memory_space=pltpu.VMEM)
    dma = pltpu.SemaphoreType.DMA
    regular = pltpu.SemaphoreType.REGULAR
    result = pl.pallas_call(
        moe_kernel,
        out_shape=jax.ShapeDtypeStruct((rows, width), BF),
        in_specs=[hbm, vmem, hbm, hbm],
        out_specs=vmem,
        scratch_shapes=[
            pltpu.VMEM((2, 2, 4, 4, ROWS, EXT + width), BF),
            pltpu.VMEM((groups, ROWS, width), BF),
            pltpu.VMEM((groups, ROWS, EXT), BF),
            pltpu.VMEM((width, 2 * units), BF),
            pltpu.VMEM((units, width), BF),
            pltpu.VMEM((32 * ROWS, 2 * units), F32),
            pltpu.VMEM((32 * ROWS, units), BF),
            pltpu.VMEM((2, 4, 4, ROWS, width), BF),
            pltpu.VMEM((4, 4, ROWS, width), BF),
            pltpu.VMEM((groups, 4, 3, 4, ROWS, quarter), BF),
            pltpu.VMEM((4, 4, ROWS, quarter), BF),
            pltpu.VMEM((groups, 4, 3, ROWS, quarter), BF),
            dma((2,)), dma((groups,)), dma((groups,)),
            dma((groups, 17)), dma((groups, 5)),
            dma((groups, 4)), dma((groups,)),
            dma((groups, 4)), dma((groups, 4)), dma((groups,)),
            dma((groups, 4)), dma((groups, 4)), dma((groups,)),
            regular((groups,)), regular((groups,)),
        ],
        compiler_params=pltpu.CompilerParams(
            collective_id=0, has_side_effects=True, vmem_limit_bytes=66_000_000
        ),
        name="moe",
    )(section_out[0], gates, gate_up, w_down[0, 0])
    return result[None]


def solution(mesh):
    return jax.shard_map(
        on_device,
        mesh=mesh,
        in_specs=(
            P("section", ("ex", "ey"), None),
            P("section", ("ex", "ey"), None),
            P("section", ("ex", "ey"), None),
            P("section", "ey", None, None, "ex"),
            P("section", "ey", "ex", None),
        ),
        out_specs=P("section", ("ex", "ey"), None),
        check_vma=False,
    )
```

time: 364 us -> 223 us (0.61)
  waiting for transfers between devices: 257 us -> 0 us
  Pallas kernels: 0 us -> 209 us
  blocking collectives: 39 us -> 0 us
  matrix products: 20.2 us -> 0 us
  between operations: 13.5 us -> 0.01 us
  local copies, waits for them, and re-layouts: 21.7 us -> 9.66 us
  starting transfers between devices: 7.64 us -> 0 us
    pallas_call x0 -> x1, Pallas kernels: none -> 209 us  [on_device(): pl.pallas_call(moe_kernel, out_shape=jax.ShapeDtypeStruct((rows, width),...]
    reduce_scatter x1 -> x0, waiting for transfers between devices: 106 us -> none  [on_device(): lax.psum_scatter(jnp.dot(hidden_all, down_rows, preferred_element_type=jn...]
    all_gather x1 -> x0, waiting for transfers between devices: 98.6 us -> none  [on_device(): lax.all_gather(arrived, 'ex', axis=0, tiled=True)]
    all_to_all x1 -> x0, blocking collectives: 39 us -> none  [on_device(): lax.all_to_all(outgoing.reshape(experts, capacity, model_width), 'ey', sp...]
    all_to_all x1 -> x0, waiting for transfers between devices: 33.2 us -> none  [on_device(): lax.all_to_all(summed.reshape(experts, capacity, model_width), 'ey', spli...]
    dot_general x3 -> x0, matrix products: 20.2 us -> none  [the longest x1 10.9 us: expert_hidden(): mixed = jnp.dot(token_rows, gate_up, preferred_element_type=jnp.float32)]
    ppermute x1 -> x0, waiting for transfers between devices: 19.8 us -> none  [shifted(): return lax.ppermute(value, axis, pairs)]
    gather x2 -> x0, local copies, waits for them, and re-layouts: 9.35 us -> none  [the longest x1 5.5 us: on_device(): picked = expert_out[position].reshape(tok_rows, top_count, model_width)]
  transfers between devices with their start and end apart: 4 -> 0, of which waited for: 4 -> 0; matrix products, arithmetic and copies ran while one was open for 3% -> 0% of each run, Pallas kernels for 0% -> 0%
where the time goes in v1:
time: 223 us; the launch traced here: 220 us
  Pallas kernels  209 us (94%)
  local copies, waits for them, and re-layouts  9.66 us (4%)
    pallas_call x1, Pallas kernels, on_device(): pl.pallas_call(moe_kernel, out_shape=jax.ShapeDtypeStruct((rows, width),...  209 us
    unnamed x2, local copies, waits for them, and re-layouts  9.5 us

profile of v1, /device:TPU:1, one launch (start us, length us, event | category | flops | bytes accessed | tf_op | source)
XLA Modules:
  0.0 220.5 jit_solution(4578709695580432855)
XLA Ops:
  0.0 0.1 pad.3.clone
  0.1 0.7 select_reduce_fusion
  0.8 0.1 copy.8
  0.9 0.7 maximum_maximum_fusion.gate_ref
  1.6 7.3 %copy.11 = bf16[896,8,2,256]{3,1,2,0:T(8,128)(2,1)} copy(bf16[896,8,2,256]{3,2,1,0:T(2,128)(2,1)} %bitcast.9) | data formatting | bytes 14680064
  8.9 209.4 %moe.1 = bf16[64,7168]{1,0:T(8,128)(2,1)} custom-call(bf16[64,7168]{1,0:T(8,128)(2,1)} %bitcast.12, f32[64,128]{1,0:T(8,128)} %maximum_maximum_fusion.gate_ref, bf16[7168,512]{1,0:T(8,128)(2,1)} %bitcast.8, bf16[256,7168]{1,0:T(8,128)(2,1)} %bitcast.11), custom_call_target="tpu_custom_call" | custom-call | tf_op jit(solution)/shard_map/moe/pallas_call | solution.py:360
  218.3 2.2 copy.13
  (1 shorter events, 0.0 us)

commit v2 on v1

--- a/solution.py
+++ b/solution.py
@@ -13,8 +13,8 @@
 
 
 def moe_kernel(
-    sec_ref, gate_ref, wgu_hbm, wd_hbm, out_ref,
-    xb, zin, ext, wgu, wd, acc, hid, part, peer, rb, tot, rb2,
+    sec_ref, id_ref, gate_ref, wgu_hbm, wd_hbm, out_ref,
+    xb, zin, ext, raw, wgu, wd, acc, hid, part, peer, rb, tot, rb2,
     wsem, zsend, zrecv, agr, ags, prd, pds, relay, meet, rsend, relay2, meet2, rsend2, free_x, free_p,
 ):
     groups = zin.shape[0]
@@ -58,19 +58,47 @@
         pl.semaphore_signal(barrier, inc=1, device_id=device, device_id_type=MESH)
     pl.semaphore_wait(barrier, 7)
 
-    for g in range(groups):
-        rdma(sec_ref.at[pl.ds(g * ROWS, ROWS)], zin.at[g], zsend.at[g], zrecv.at[g], to_zp).start()
-    load_gu = pltpu.make_async_copy(wgu_hbm, wgu, wsem.at[0])
-    load_d = pltpu.make_async_copy(wd_hbm, wd, wsem.at[1])
-    load_gu.start()
+    def relay_rows(g):
+        rows = pl.ds(pl.multiple_of(g * ROWS, ROWS), ROWS)
+        return rdma(sec_ref.at[rows], zin.at[g], zsend.at[g], zrecv.at[g], to_zp)
+
+    relay_rows(0).start()
+    pieces, piece = width // raw.shape[1], raw.shape[1]
+
+    def load(k, slot):
+        return pltpu.make_async_copy(wgu_hbm.at[pl.ds(k * piece, piece)], raw.at[slot], wsem.at[slot])
+
+    load(0, 0).start()
+    load(1, 1).start()
+    load_d = pltpu.make_async_copy(wd_hbm, wd, wsem.at[2])
     load_d.start()
 
-    gate = gate_ref[...]
-    high = gate.astype(BF).astype(F32)
-    mid = (gate - high).astype(BF).astype(F32)
-    low = gate - high - mid
-    lane = lax.broadcasted_iota(jnp.int32, gate.shape, 1)
-    ext[...] = jnp.where(lane < 8, high, jnp.where(lane < 16, mid, low)).astype(BF).reshape(ext.shape)
+    row = lax.broadcasted_iota(jnp.int32, (EXT, EXT), 0)
+    table = jnp.zeros((EXT, EXT), F32)
+    ids = jnp.concatenate([id_ref[...]] * (EXT // id_ref.shape[1]), axis=1)
+    weights = jnp.concatenate([gate_ref[...]] * (EXT // gate_ref.shape[1]), axis=1)
+    for k in range(ids.shape[0]):
+        table = table + jnp.where(lax.rem(row, 8) == ids[k : k + 1], weights[k : k + 1], 0.0)
+    high = table.astype(BF).astype(F32)
+    mid = (table - high).astype(BF).astype(F32)
+    low = table - high - mid
+    terms = jnp.where(row < 8, high, jnp.where(row < 16, mid, jnp.where(row < 24, low, 0.0)))
+    ext[...] = terms.T[: groups * ROWS].astype(BF).reshape(ext.shape)
+
+    def unpack(first, count):
+        for k in range(first, first + count):
+            slot = k % 2
+            load(k, slot).wait()
+
+            def step(j, carry):
+                at = pl.multiple_of(j * 128, 128)
+                to = pl.multiple_of(k * piece + j * 128, 128)
+                wgu[pl.ds(to, 128), :] = raw[slot, pl.ds(at, 128)].reshape(128, wgu.shape[1])
+                return carry
+
+            lax.fori_loop(0, piece // 128, step, 0)
+            if k + 2 < pieces:
+                load(k + 2, slot).start()
 
     def gather_1(a, p):
         @pl.when(a >= 2)
@@ -78,6 +106,11 @@
             pl.semaphore_wait(free_x.at[a - 2], 5)
 
         wait_recv(zin.at[a], zrecv.at[a])
+
+        @pl.when(a + 1 < groups)
+        def _():
+            relay_rows(a + 1).start()
+
         own = xb.at[p, c, y, x]
         own[:, pl.ds(0, EXT)] = ext[a]
         own[:, pl.ds(EXT, width)] = zin[a]
@@ -198,36 +231,41 @@
     dev_first = ((to_yp, to_ym), (to_ym, to_yp), (to_xp, to_xm), (to_xm, to_xp))
     dev_second = ((to_xp, to_xm), (to_xm, to_xp), (to_yp, to_ym), (to_ym, to_yp))
 
-    def wait_part(g):
-        wait_send(part.at[co], pds.at[g])
-        wait_send(part.at[c, pl.ds(0, 3)], rsend.at[g])
-
     def down(g):
         @pl.when(g >= 1)
         def _():
-            wait_part(g - 1)
+            wait_send(part.at[co], pds.at[g - 1])
             pl.semaphore_wait(free_p.at[g - 1], 1)
 
         tile = 256
+        side = tokens // 2
+        rows_peer = pl.ds(pl.multiple_of(co * side, side), side)
+        rows_mine = pl.ds(pl.multiple_of(c * side, side), side)
         for q in range(4):
             def step(j, carry):
                 at = pl.multiple_of(q * quarter + j * tile, 128)
-                value = jnp.dot(hid[...], wd[:, pl.ds(at, tile)], preferred_element_type=F32)
-                part[:, :, :, :, pl.ds(at, tile)] = value.astype(BF).reshape(2, 4, 4, ROWS, tile)
+                value = jnp.dot(hid[rows_peer, :], wd[:, pl.ds(at, tile)], preferred_element_type=F32)
+                part[co, :, :, :, pl.ds(at, tile)] = value.astype(BF).reshape(4, 4, ROWS, tile)
                 return carry
 
             lax.fori_loop(0, quarter // tile, step, 0)
             rdma(part.at[co, :, :, :, cols(q)], peer.at[:, :, :, cols(q)], pds.at[g], prd.at[g, q], to_peer).start()
+
+        @pl.when(g >= 1)
+        def _():
+            wait_send(part.at[c, pl.ds(0, 3)], rsend.at[g - 1])
+
         for q in range(4):
             wait_recv(peer.at[:, :, :, cols(q)], prd.at[g, q])
 
-            def add(i, carry):
-                iy, ix = lax.div(i, 4), lax.rem(i, 4)
-                total = part[c, iy, ix, :, cols(q)].astype(F32) + peer[iy, ix, :, cols(q)].astype(F32)
-                part[c, iy, ix, :, cols(q)] = total.astype(BF)
+            def add(j, carry):
+                at = pl.multiple_of(q * quarter + j * tile, 128)
+                value = jnp.dot(hid[rows_mine, :], wd[:, pl.ds(at, tile)], preferred_element_type=F32)
+                value = value + peer[:, :, :, pl.ds(at, tile)].reshape(side, tile).astype(F32)
+                part[c, :, :, :, pl.ds(at, tile)] = value.astype(BF).reshape(4, 4, ROWS, tile)
                 return carry
 
-            lax.fori_loop(0, 16, add, 0)
+            lax.fori_loop(0, quarter // tile, add, 0)
             k = q % 2
             rdma(pick(q, xd, yd), rb.at[g, q, 0], rsend.at[g], relay.at[g, q], dev_first[q][0]).start()
             rdma(pick(q, *bwd[k]), rb.at[g, q, 1], rsend.at[g], meet.at[g, q], dev_first[q][1]).start()
@@ -281,65 +319,66 @@
         wait_send(tot.at[pl.ds(0, 3)], rsend2.at[g])
 
     def turn(i, carry):
-        a, g, t = i, i - 1, i - 2
-        pa, pg = lax.rem(a, 2), lax.rem(i + 1, 2)
-        gathers = a < groups
+        a, n, g, t = i, i + 1, i - 1, i - 2
+        pa, pn = lax.rem(i, 2), lax.rem(i + 1, 2)
+        gathers, starts = a < groups, n < groups
         computes = (g >= 0) & (g < groups)
         ends = t >= 0
 
-        @pl.when(i == 1)
-        def _():
-            load_gu.wait()
-            load_d.wait()
+        @pl.when(computes)
+        def _():
+            up(g, pn)
 
         @pl.when(gathers)
         def _():
-            gather_1(a, pa)
+            gather_3(a, pa)
+
+        @pl.when(ends)
+        def _():
+            scatter_3(t)
 
         @pl.when(computes)
         def _():
-            up(g, pg)
+            down(g)
+
+        @pl.when(gathers)
+        def _():
+            gather_4(a, pa)
 
         @pl.when(ends)
         def _():
-            scatter_3(t)
+            scatter_4(t)
+
+        @pl.when(starts)
+        def _():
+            gather_1(n, pn)
+
+        @pl.when(computes)
+        def _():
+            scatter_2(g)
+
+        @pl.when(ends)
+        def _():
+            scatter_5(t)
 
         @pl.when(gathers)
         def _():
-            gather_2(a, pa)
-
-        @pl.when(computes)
-        def _():
-            down(g)
-
-        @pl.when(ends)
-        def _():
-            scatter_4(t)
-
-        @pl.when(gathers)
-        def _():
-            gather_3(a, pa)
-
-        @pl.when(ends)
-        def _():
-            scatter_5(t)
-
-        @pl.when(gathers)
-        def _():
-            gather_4(a, pa)
-
-        @pl.when(computes)
-        def _():
-            scatter_2(g)
-
-        @pl.when(gathers)
-        def _():
             gather_5(a, pa)
 
+        @pl.when(starts)
+        def _():
+            gather_2(n, pn)
+
         return carry
 
+    gather_1(0, 0)
+    unpack(0, pieces // 2)
+    gather_2(0, 0)
+    unpack(pieces // 2, pieces - pieces // 2)
+    load_d.wait()
     lax.fori_loop(0, groups + 2, turn, 0)
-    wait_part(groups - 1)
+    wait_send(part.at[co], pds.at[groups - 1])
+    wait_send(part.at[c, pl.ds(0, 3)], rsend.at[groups - 1])
     for g in range(groups):
         wait_send(zin.at[g], zsend.at[g])
 
@@ -349,10 +388,6 @@
     units = w_down.shape[2]
     groups = rows // ROWS
     quarter = width // 4
-    chosen = expert_ids[0][:, :, None] == jnp.arange(8, dtype=jnp.int32)[None, None, :]
-    dense = jnp.sum(jnp.where(chosen, gate_weights[0][:, :, None], 0.0), axis=1)
-    gates = jnp.concatenate([dense, dense, dense, jnp.zeros((rows, EXT - 24), F32)], axis=1)
-    gate_up = w_gate_up[0, 0].reshape(width, 2 * units)
     hbm = pl.BlockSpec(memory_space=pl.ANY)
     vmem = pl.BlockSpec(memory_space=pltpu.VMEM)
     dma = pltpu.SemaphoreType.DMA
@@ -360,12 +395,13 @@
     result = pl.pallas_call(
         moe_kernel,
         out_shape=jax.ShapeDtypeStruct((rows, width), BF),
-        in_specs=[hbm, vmem, hbm, hbm],
+        in_specs=[hbm, vmem, vmem, hbm, hbm],
         out_specs=vmem,
         scratch_shapes=[
             pltpu.VMEM((2, 2, 4, 4, ROWS, EXT + width), BF),
             pltpu.VMEM((groups, ROWS, width), BF),
             pltpu.VMEM((groups, ROWS, EXT), BF),
+            pltpu.VMEM((2, width // 8, 2, units), BF),
             pltpu.VMEM((width, 2 * units), BF),
             pltpu.VMEM((units, width), BF),
             pltpu.VMEM((32 * ROWS, 2 * units), F32),
@@ -375,7 +411,7 @@
             pltpu.VMEM((groups, 4, 3, 4, ROWS, quarter), BF),
             pltpu.VMEM((4, 4, ROWS, quarter), BF),
             pltpu.VMEM((groups, 4, 3, ROWS, quarter), BF),
-            dma((2,)), dma((groups,)), dma((groups,)),
+            dma((3,)), dma((groups,)), dma((groups,)),
             dma((groups, 17)), dma((groups, 5)),
             dma((groups, 4)), dma((groups,)),
             dma((groups, 4)), dma((groups, 4)), dma((groups,)),
@@ -386,7 +422,7 @@
             collective_id=0, has_side_effects=True, vmem_limit_bytes=66_000_000
         ),
         name="moe",
-    )(section_out[0], gates, gate_up, w_down[0, 0])
+    )(section_out[0], expert_ids[0].T, gate_weights[0].T, w_gate_up[0, 0], w_down[0, 0])
     return result[None]
 
 

time: 223 us -> 207 us (0.928)
  local copies, waits for them, and re-layouts: 9.66 us -> 2.16 us
  Pallas kernels: 209 us -> 204 us
    unnamed x2 -> x1, local copies, waits for them, and re-layouts: 9.5 us -> 2.16 us
    pallas_call x1, Pallas kernels: 209 us -> 204 us  [on_device(): pl.pallas_call(moe_kernel, out_shape=jax.ShapeDtypeStruct((rows, width),...]
where the time goes in v2:
time: 207 us; the launch traced here: 206 us
  Pallas kernels  204 us (99%)
  local copies, waits for them, and re-layouts  2.16 us (1%)
    pallas_call x1, Pallas kernels, on_device(): pl.pallas_call(moe_kernel, out_shape=jax.ShapeDtypeStruct((rows, width),...  204 us

profile of v2, /device:TPU:1, one launch (start us, length us, event | category | flops | bytes accessed | tf_op | source)
XLA Modules:
  0.0 206.4 jit_solution(3906084216001681027)
XLA Ops:
  0.0 204.3 %moe.1 = bf16[64,7168]{1,0:T(8,128)(2,1)} custom-call(bf16[64,7168]{1,0:T(8,128)(2,1)} %bitcast.13, s32[2,64]{1,0:T(2,128)} %bitcast.14, f32[2,64]{1,0:T(2,128)} %bitcast.15, bf16[7168,2,256]{2,1,0:T(2,128)(2,1)} %bitcast.10, bf16[256,7168]{1,0:T(8,128)(2,1)} %bitcast.12), custom_call_target="tpu_custom_call" | custom-call | tf_op jit(solution)/shard_map/moe/pallas_call | solution.py:395
  204.3 2.2 %copy.7 = bf16[1,64,7168]{2,1,0:T(8,128)(2,1)} copy(bf16[1,64,7168]{2,1,0:T(8,128)(2,1)} %bitcast.11) | data formatting | bytes 1835008

commit v3 on v2

--- a/solution.py
+++ b/solution.py
@@ -182,7 +182,7 @@
         to_partner(a, across.at[:, :, col_b])
 
     tokens = acc.shape[0]
-    depth = quarter if quarter % 256 else quarter // 2
+    depth = quarter
 
     def up(g, p):
         wait_recv(xb.at[p, co], agr.at[g, 16])
@@ -231,16 +231,16 @@
     dev_first = ((to_yp, to_ym), (to_ym, to_yp), (to_xp, to_xm), (to_xm, to_xp))
     dev_second = ((to_xp, to_xm), (to_xm, to_xp), (to_yp, to_ym), (to_ym, to_yp))
 
-    def down(g):
+    tile = 256
+    side = tokens // 2
+
+    def down_peer(g):
         @pl.when(g >= 1)
         def _():
             wait_send(part.at[co], pds.at[g - 1])
             pl.semaphore_wait(free_p.at[g - 1], 1)
 
-        tile = 256
-        side = tokens // 2
         rows_peer = pl.ds(pl.multiple_of(co * side, side), side)
-        rows_mine = pl.ds(pl.multiple_of(c * side, side), side)
         for q in range(4):
             def step(j, carry):
                 at = pl.multiple_of(q * quarter + j * tile, 128)
@@ -248,12 +248,15 @@
                 part[co, :, :, :, pl.ds(at, tile)] = value.astype(BF).reshape(4, 4, ROWS, tile)
                 return carry
 
-            lax.fori_loop(0, quarter // tile, step, 0)
+            lax.fori_loop(0, quarter // tile, step, 0, unroll=True)
             rdma(part.at[co, :, :, :, cols(q)], peer.at[:, :, :, cols(q)], pds.at[g], prd.at[g, q], to_peer).start()
 
+    def down_mine(g):
         @pl.when(g >= 1)
         def _():
             wait_send(part.at[c, pl.ds(0, 3)], rsend.at[g - 1])
+
+        rows_mine = pl.ds(pl.multiple_of(c * side, side), side)
 
         for q in range(4):
             wait_recv(peer.at[:, :, :, cols(q)], prd.at[g, q])
@@ -265,10 +268,10 @@
                 part[c, :, :, :, pl.ds(at, tile)] = value.astype(BF).reshape(4, 4, ROWS, tile)
                 return carry
 
-            lax.fori_loop(0, quarter // tile, add, 0)
-            k = q % 2
+            lax.fori_loop(0, quarter // tile, add, 0, unroll=True)
             rdma(pick(q, xd, yd), rb.at[g, q, 0], rsend.at[g], relay.at[g, q], dev_first[q][0]).start()
-            rdma(pick(q, *bwd[k]), rb.at[g, q, 1], rsend.at[g], meet.at[g, q], dev_first[q][1]).start()
+        for q in range(4):
+            rdma(pick(q, *bwd[q % 2]), rb.at[g, q, 1], rsend.at[g], meet.at[g, q], dev_first[q][1]).start()
 
         @pl.when(g < groups - 1)
         def _():
@@ -297,9 +300,10 @@
                 return carry
 
             lax.fori_loop(0, 4, add, 0)
-            k = q % 2
-            far, back = (xd, bwd[k][0]) if q < 2 else (yd, bwd[k][1])
+            far = xd if q < 2 else yd
             rdma(tot.at[q, far], rb2.at[g, q, 0], rsend2.at[g], relay2.at[g, q], dev_second[q][0]).start()
+        for q in range(4):
+            back = bwd[q % 2][0] if q < 2 else bwd[q % 2][1]
             rdma(tot.at[q, back], rb2.at[g, q, 1], rsend2.at[g], meet2.at[g, q], dev_second[q][1]).start()
 
     def scatter_4(g):
@@ -319,64 +323,35 @@
         wait_send(tot.at[pl.ds(0, 3)], rsend2.at[g])
 
     def turn(i, carry):
-        a, n, g, t = i, i + 1, i - 1, i - 2
-        pa, pn = lax.rem(i, 2), lax.rem(i + 1, 2)
-        gathers, starts = a < groups, n < groups
-        computes = (g >= 0) & (g < groups)
-        ends = t >= 0
-
-        @pl.when(computes)
-        def _():
-            up(g, pn)
-
-        @pl.when(gathers)
-        def _():
-            gather_3(a, pa)
-
-        @pl.when(ends)
-        def _():
-            scatter_3(t)
-
-        @pl.when(computes)
-        def _():
-            down(g)
-
-        @pl.when(gathers)
-        def _():
-            gather_4(a, pa)
-
-        @pl.when(ends)
-        def _():
-            scatter_4(t)
-
-        @pl.when(starts)
-        def _():
-            gather_1(n, pn)
-
-        @pl.when(computes)
-        def _():
-            scatter_2(g)
-
-        @pl.when(ends)
-        def _():
-            scatter_5(t)
-
-        @pl.when(gathers)
-        def _():
-            gather_5(a, pa)
-
-        @pl.when(starts)
-        def _():
-            gather_2(n, pn)
-
+        def stage(act, g, *rest):
+            @pl.when((g >= 0) & (g < groups))
+            def _():
+                act(g, *rest)
+
+        here, other = lax.rem(i, 2), lax.rem(i + 1, 2)
+        stage(gather_4, i - 1, other)
+        stage(scatter_3, i - 3)
+        stage(down_mine, i - 2)
+        stage(gather_2, i, here)
+
+        @pl.when(i == 0)
+        def _():
+            unpack(pieces // 2, pieces - pieces // 2)
+            load_d.wait()
+
+        stage(gather_5, i - 1, other)
+        stage(gather_3, i, here)
+        stage(scatter_4, i - 3)
+        stage(up, i - 1, other)
+        stage(scatter_2, i - 2)
+        stage(scatter_5, i - 3)
+        stage(gather_1, i + 1, other)
+        stage(down_peer, i - 1)
         return carry
 
     gather_1(0, 0)
     unpack(0, pieces // 2)
-    gather_2(0, 0)
-    unpack(pieces // 2, pieces - pieces // 2)
-    load_d.wait()
-    lax.fori_loop(0, groups + 2, turn, 0)
+    lax.fori_loop(0, groups + 3, turn, 0)
     wait_send(part.at[co], pds.at[groups - 1])
     wait_send(part.at[c, pl.ds(0, 3)], rsend.at[groups - 1])
     for g in range(groups):
@@ -419,7 +394,7 @@
             regular((groups,)), regular((groups,)),
         ],
         compiler_params=pltpu.CompilerParams(
-            collective_id=0, has_side_effects=True, vmem_limit_bytes=66_000_000
+            collective_id=0, has_side_effects=True, vmem_limit_bytes=62_000_000
         ),
         name="moe",
     )(section_out[0], expert_ids[0].T, gate_weights[0].T, w_gate_up[0, 0], w_down[0, 0])

time: 207 us -> 185 us (0.89)
  Pallas kernels: 204 us -> 181 us
    pallas_call x1, Pallas kernels: 204 us -> 181 us  [on_device(): pl.pallas_call(moe_kernel, out_shape=jax.ShapeDtypeStruct((rows, width),...]
where the time goes in v3:
time: 185 us; the launch traced here: 183 us
  Pallas kernels  181 us (98%)
  local copies, waits for them, and re-layouts  2.16 us (1%)
    pallas_call x1, Pallas kernels, on_device(): pl.pallas_call(moe_kernel, out_shape=jax.ShapeDtypeStruct((rows, width),...  181 us

profile of v3, /device:TPU:1, one launch (start us, length us, event | category | flops | bytes accessed | tf_op | source)
XLA Modules:
  0.0 183.2 jit_solution(6303798781004890673)
XLA Ops:
  0.0 181.1 %moe.1 = bf16[64,7168]{1,0:T(8,128)(2,1)} custom-call(bf16[64,7168]{1,0:T(8,128)(2,1)} %bitcast.13, s32[2,64]{1,0:T(2,128)} %bitcast.14, f32[2,64]{1,0:T(2,128)} %bitcast.15, bf16[7168,2,256]{2,1,0:T(2,128)(2,1)} %bitcast.10, bf16[256,7168]{1,0:T(8,128)(2,1)} %bitcast.12), custom_call_target="tpu_custom_call" | custom-call | tf_op jit(solution)/shard_map/moe/pallas_call | solution.py:370
  181.1 2.2 %copy.7 = bf16[1,64,7168]{2,1,0:T(8,128)(2,1)} copy(bf16[1,64,7168]{2,1,0:T(8,128)(2,1)} %bitcast.11) | data formatting | bytes 1835008

commit v4 on v3

--- a/solution.py
+++ b/solution.py
@@ -14,8 +14,8 @@
 
 def moe_kernel(
     sec_ref, id_ref, gate_ref, wgu_hbm, wd_hbm, out_ref,
-    xb, zin, ext, raw, wgu, wd, acc, hid, part, peer, rb, tot, rb2,
-    wsem, zsend, zrecv, agr, ags, prd, pds, relay, meet, rsend, relay2, meet2, rsend2, free_x, free_p,
+    xb, zin, zout, ext, raw, wgu, wd, acc, hid, part, peer, rb, tot, rb2,
+    wsem, zsend, zrecv, agr, ags, prd, pds, relay, meet, comb, rsend, relay2, meet2, rsend2, free_x, free_p,
 ):
     groups = zin.shape[0]
     width = zin.shape[2]
@@ -53,6 +53,8 @@
     def wait_send(ref, sem):
         rdma(ref, ref, sem, sem, to_peer).wait_send()
 
+    stage_0 = pltpu.make_async_copy(sec_ref.at[pl.ds(0, ROWS)], zout, wsem.at[3])
+    stage_0.start()
     barrier = pltpu.get_barrier_semaphore()
     for device in (to_xp, to_xm, to_yp, to_ym, to_peer, to_zp, to_zm):
         pl.semaphore_signal(barrier, inc=1, device_id=device, device_id_type=MESH)
@@ -62,7 +64,8 @@
         rows = pl.ds(pl.multiple_of(g * ROWS, ROWS), ROWS)
         return rdma(sec_ref.at[rows], zin.at[g], zsend.at[g], zrecv.at[g], to_zp)
 
-    relay_rows(0).start()
+    stage_0.wait()
+    rdma(zout, zin.at[0], zsend.at[0], zrecv.at[0], to_zp).start()
     pieces, piece = width // raw.shape[1], raw.shape[1]
 
     def load(k, slot):
@@ -277,6 +280,10 @@
         def _():
             pl.semaphore_signal(free_p.at[g], inc=1, device_id=to_peer, device_id_type=MESH)
 
+    def turns(q):
+        k = q // 2
+        return ((xd, yd)[k], bwd[q % 2][k], fwd[q % 2][k], (x, y)[k])
+
     def scatter_2(g):
         for q in range(4):
             wait_recv(rb.at[g, q, 0], relay.at[g, q])
@@ -287,24 +294,26 @@
                 return carry
 
             lax.fori_loop(0, 4, add, 0)
-            rdma(mine, rb.at[g, q, 2], rsend.at[g], meet.at[g, q], dev_first[q][0]).start()
+            for k, at in enumerate(turns(q)):
+                rdma(mine.at[at], rb.at[g, q, 2, at], rsend.at[g], comb.at[g, q, k], dev_first[q][0]).start()
 
     def scatter_3(g):
-        for q in range(4):
-            wait_recv(rb.at[g, q, pl.ds(1, 2)], meet.at[g, q])
+        def settle(q, k):
+            at = turns(q)[k]
+            wait_recv(rb.at[g, q, 2, at], comb.at[g, q, k])
             mine = pick(q, x, y)
-
-            def add(i, carry):
-                total = mine[i].astype(F32) + rb[g, q, 1, i].astype(F32) + rb[g, q, 2, i].astype(F32)
-                tot[q, i] = total.astype(BF)
-                return carry
-
-            lax.fori_loop(0, 4, add, 0)
-            far = xd if q < 2 else yd
-            rdma(tot.at[q, far], rb2.at[g, q, 0], rsend2.at[g], relay2.at[g, q], dev_second[q][0]).start()
-        for q in range(4):
-            back = bwd[q % 2][0] if q < 2 else bwd[q % 2][1]
-            rdma(tot.at[q, back], rb2.at[g, q, 1], rsend2.at[g], meet2.at[g, q], dev_second[q][1]).start()
+            total = mine[at].astype(F32) + rb[g, q, 1, at].astype(F32) + rb[g, q, 2, at].astype(F32)
+            tot[q, at] = total.astype(BF)
+            return tot.at[q, at]
+
+        for q in range(4):
+            wait_recv(rb.at[g, q, 1], meet.at[g, q])
+            rdma(settle(q, 0), rb2.at[g, q, 0], rsend2.at[g], relay2.at[g, q], dev_second[q][0]).start()
+        for q in range(4):
+            rdma(settle(q, 1), rb2.at[g, q, 1], rsend2.at[g], meet2.at[g, q], dev_second[q][1]).start()
+        for q in range(4):
+            settle(q, 2)
+            settle(q, 3)
 
     def scatter_4(g):
         for q in range(4):
@@ -331,7 +340,6 @@
         here, other = lax.rem(i, 2), lax.rem(i + 1, 2)
         stage(gather_4, i - 1, other)
         stage(scatter_3, i - 3)
-        stage(down_mine, i - 2)
         stage(gather_2, i, here)
 
         @pl.when(i == 0)
@@ -339,14 +347,15 @@
             unpack(pieces // 2, pieces - pieces // 2)
             load_d.wait()
 
+        stage(down_mine, i - 2)
         stage(gather_5, i - 1, other)
         stage(gather_3, i, here)
         stage(scatter_4, i - 3)
         stage(up, i - 1, other)
         stage(scatter_2, i - 2)
-        stage(scatter_5, i - 3)
         stage(gather_1, i + 1, other)
         stage(down_peer, i - 1)
+        stage(scatter_5, i - 3)
         return carry
 
     gather_1(0, 0)
@@ -375,6 +384,7 @@
         scratch_shapes=[
             pltpu.VMEM((2, 2, 4, 4, ROWS, EXT + width), BF),
             pltpu.VMEM((groups, ROWS, width), BF),
+            pltpu.VMEM((ROWS, width), BF),
             pltpu.VMEM((groups, ROWS, EXT), BF),
             pltpu.VMEM((2, width // 8, 2, units), BF),
             pltpu.VMEM((width, 2 * units), BF),
@@ -386,15 +396,15 @@
             pltpu.VMEM((groups, 4, 3, 4, ROWS, quarter), BF),
             pltpu.VMEM((4, 4, ROWS, quarter), BF),
             pltpu.VMEM((groups, 4, 3, ROWS, quarter), BF),
-            dma((3,)), dma((groups,)), dma((groups,)),
+            dma((4,)), dma((groups,)), dma((groups,)),
             dma((groups, 17)), dma((groups, 5)),
             dma((groups, 4)), dma((groups,)),
-            dma((groups, 4)), dma((groups, 4)), dma((groups,)),
+            dma((groups, 4)), dma((groups, 4)), dma((groups, 4, 4)), dma((groups,)),
             dma((groups, 4)), dma((groups, 4)), dma((groups,)),
             regular((groups,)), regular((groups,)),
         ],
         compiler_params=pltpu.CompilerParams(
-            collective_id=0, has_side_effects=True, vmem_limit_bytes=62_000_000
+            collective_id=0, has_side_effects=True, vmem_limit_bytes=58_500_000
         ),
         name="moe",
     )(section_out[0], expert_ids[0].T, gate_weights[0].T, w_gate_up[0, 0], w_down[0, 0])

time: 185 us -> 181 us (0.978)
  Pallas kernels: 181 us -> 179 us
    pallas_call x1, Pallas kernels: 181 us -> 179 us  [on_device(): pl.pallas_call(moe_kernel, out_shape=jax.ShapeDtypeStruct((rows, width),...]
where the time goes in v4:
time: 181 us
  Pallas kernels  179 us (99%)
  local copies, waits for them, and re-layouts  2.16 us (1%)
    pallas_call x1, Pallas kernels, on_device(): pl.pallas_call(moe_kernel, out_shape=jax.ShapeDtypeStruct((rows, width),...  179 us

profile of v4, /device:TPU:1, one launch (start us, length us, event | category | flops | bytes accessed | tf_op | source)
XLA Modules:
  0.0 181.0 jit_solution(3115062707140616920)
XLA Ops:
  0.0 178.8 %moe.1 = bf16[64,7168]{1,0:T(8,128)(2,1)} custom-call(bf16[64,7168]{1,0:T(8,128)(2,1)} %bitcast.13, s32[2,64]{1,0:T(2,128)} %bitcast.14, f32[2,64]{1,0:T(2,128)} %bitcast.15, bf16[7168,2,256]{2,1,0:T(2,128)(2,1)} %bitcast.10, bf16[256,7168]{1,0:T(8,128)(2,1)} %bitcast.12), custom_call_target="tpu_custom_call" | custom-call | tf_op jit(solution)/shard_map/moe/pallas_call | solution.py:379
  178.8 2.2 %copy.7 = bf16[1,64,7168]{2,1,0:T(8,128)(2,1)} copy(bf16[1,64,7168]{2,1,0:T(8,128)(2,1)} %bitcast.11) | data formatting | bytes 1835008

commit v5 on v4

--- a/solution.py
+++ b/solution.py
@@ -65,7 +65,9 @@
         return rdma(sec_ref.at[rows], zin.at[g], zsend.at[g], zrecv.at[g], to_zp)
 
     stage_0.wait()
-    rdma(zout, zin.at[0], zsend.at[0], zrecv.at[0], to_zp).start()
+    first, last = pl.ds(0, 2 * quarter), pl.ds(2 * quarter, 2 * quarter)
+    rdma(zout.at[:, first], zin.at[0, :, first], zsend.at[0], zrecv.at[0], to_zp).start()
+    rdma(zout.at[:, last], zin.at[0, :, last], zsend.at[0], zrecv.at[groups], to_zp).start()
     pieces, piece = width // raw.shape[1], raw.shape[1]
 
     def load(k, slot):
@@ -124,6 +126,25 @@
         rdma(own_b, own_b, ags.at[a, 0], agr.at[a, 3], to_ym).start()
         rdma(own, own, ags.at[a, 4], agr.at[a, 16], to_peer).start()
         spread(a, p, x, y)
+
+    def gather_1_first():
+        own = xb.at[0, c, y, x]
+        own_a, own_b = own.at[:, col_a], own.at[:, col_b]
+        wait_recv(zin.at[0, :, first], zrecv.at[0])
+        own[:, pl.ds(0, EXT)] = ext[0]
+        own[:, pl.ds(EXT, 2 * quarter)] = zin[0, :, first]
+        rdma(own_a, own_a, ags.at[0, 0], agr.at[0, 0], to_xp).start()
+        rdma(own_a, own_a, ags.at[0, 0], agr.at[0, 1], to_xm).start()
+        rdma(own_a, own_a, ags.at[0, 2], agr.at[0, 8], to_yp).start()
+        rdma(own_a, own_a, ags.at[0, 2], agr.at[0, 9], to_ym).start()
+        wait_recv(zin.at[0, :, last], zrecv.at[groups])
+        relay_rows(1).start()
+        own[:, col_b] = zin[0, :, last]
+        rdma(own_b, own_b, ags.at[0, 0], agr.at[0, 2], to_yp).start()
+        rdma(own_b, own_b, ags.at[0, 0], agr.at[0, 3], to_ym).start()
+        rdma(own_b, own_b, ags.at[0, 2], agr.at[0, 10], to_xp).start()
+        rdma(own_b, own_b, ags.at[0, 2], agr.at[0, 11], to_xm).start()
+        rdma(own, own, ags.at[0, 4], agr.at[0, 16], to_peer).start()
 
     def spread(a, p, bx, by):
         src_a, src_b = xb.at[p, c, y, bx, :, col_a], xb.at[p, c, by, x, :, col_b]
@@ -197,7 +218,7 @@
             acc[...] = jnp.where(k == 0, term, acc[...] + term)
             return carry
 
-        lax.fori_loop(0, width // depth, step, 0)
+        lax.fori_loop(0, width // depth, step, 0, unroll=2)
 
         def activate(i, carry):
             fours = 4 * ROWS
@@ -211,7 +232,7 @@
             hid[pl.ds(at, fours), :] = (value * weight).astype(BF)
             return carry
 
-        lax.fori_loop(0, tokens // (4 * ROWS), activate, 0)
+        lax.fori_loop(0, tokens // (4 * ROWS), activate, 0, unroll=2)
         wait_send(xb.at[p, c, 0, pl.ds(0, 2)], ags.at[g, 0])
         wait_send(xb.at[p, c, 0, 0], ags.at[g, 1])
         wait_send(xb.at[p, c, pl.ds(0, 2)], ags.at[g, 2])
@@ -351,14 +372,14 @@
         stage(gather_5, i - 1, other)
         stage(gather_3, i, here)
         stage(scatter_4, i - 3)
+        stage(scatter_2, i - 2)
         stage(up, i - 1, other)
-        stage(scatter_2, i - 2)
         stage(gather_1, i + 1, other)
         stage(down_peer, i - 1)
         stage(scatter_5, i - 3)
         return carry
 
-    gather_1(0, 0)
+    gather_1_first()
     unpack(0, pieces // 2)
     lax.fori_loop(0, groups + 3, turn, 0)
     wait_send(part.at[co], pds.at[groups - 1])
@@ -396,7 +417,7 @@
             pltpu.VMEM((groups, 4, 3, 4, ROWS, quarter), BF),
             pltpu.VMEM((4, 4, ROWS, quarter), BF),
             pltpu.VMEM((groups, 4, 3, ROWS, quarter), BF),
-            dma((4,)), dma((groups,)), dma((groups,)),
+            dma((4,)), dma((groups,)), dma((groups + 1,)),
             dma((groups, 17)), dma((groups, 5)),
             dma((groups, 4)), dma((groups,)),
             dma((groups, 4)), dma((groups, 4)), dma((groups, 4, 4)), dma((groups,)),

time: 181 us -> 180 us (level)
  no operation moved by 1% of the time
where the time goes in v5:
time: 180 us
  Pallas kernels  178 us (99%)
  local copies, waits for them, and re-layouts  2.16 us (1%)
    pallas_call x1, Pallas kernels, on_device(): pl.pallas_call(moe_kernel, out_shape=jax.ShapeDtypeStruct((rows, width),...  178 us

profile of v5, /device:TPU:1, one launch (start us, length us, event | category | flops | bytes accessed | tf_op | source)
XLA Modules:
  0.0 179.7 jit_solution(4882476348882729299)
XLA Ops:
  0.0 177.6 %moe.1 = bf16[64,7168]{1,0:T(8,128)(2,1)} custom-call(bf16[64,7168]{1,0:T(8,128)(2,1)} %bitcast.13, s32[2,64]{1,0:T(2,128)} %bitcast.14, f32[2,64]{1,0:T(2,128)} %bitcast.15, bf16[7168,2,256]{2,1,0:T(2,128)(2,1)} %bitcast.10, bf16[256,7168]{1,0:T(8,128)(2,1)} %bitcast.12), custom_call_target="tpu_custom_call" | custom-call | tf_op jit(solution)/shard_map/moe/pallas_call | solution.py:400
  177.6 2.2 %copy.7 = bf16[1,64,7168]{2,1,0:T(8,128)(2,1)} copy(bf16[1,64,7168]{2,1,0:T(8,128)(2,1)} %bitcast.11) | data formatting | bytes 1835008
